TPU v7x, 32 devices: a whole 2x2x4 slice. The times are simulated.
32 devices in a mesh: blk: 16 (over z, y, core), uly: 2 (over x).
Axes of the slice: x: 2, y: 2, z: 4, core: 2. Of those that a mesh axis runs over, the one named last changes fastest.
Arguments:
- footage_probes: bfloat16 [1024, 32, 64], P(('blk', 'uly')), may hold values from -6 to 6
- footage_lookup_keys: bfloat16 [1024, 32, 64], P(('blk', 'uly')), may hold values from -6 to 6
- footage_payload: bfloat16 [1024, 32, 64], P(('blk', 'uly')), may hold values from -6 to 6
- caption_probes: bfloat16 [256, 32, 64], replicated, may hold values from -6 to 6
- caption_lookup_keys: bfloat16 [256, 32, 64], replicated, may hold values from -6 to 6
- caption_payload: bfloat16 [256, 32, 64], replicated, may hold values from -6 to 6
- footage_probes_amplitude: float32 [64], replicated, may hold values from 0.25 to 1.75
- footage_keys_amplitude: float32 [64], replicated, may hold values from 0.25 to 1.75
- caption_probes_amplitude: float32 [64], replicated, may hold values from 0.25 to 1.75
- caption_keys_amplitude: float32 [64], replicated, may hold values from 0.25 to 1.75
- focus_sharpness: float32 [32], replicated, may hold values from 1.5 to 4
- caption_validity: int32 [256], replicated, may hold values 0 or 1
Outputs:
- vid_out: bfloat16 [1024, 32, 64], P(('blk', 'uly'))
- txt_out: bfloat16 [256, 32, 64], P('uly', 'blk')
Inputs may be any that keep to these rules, and one draw needn't show every extreme that they name: caption_validity holds only 0 and 1.
All inputs are finite; a program needn't handle non-finite values.
Results may differ from a plain program's by a relative error of at most 0.0035.
Values may be sent and summed in bfloat16 or wider, within the bound.
A program may use at most 64 MiB of HBM per device.

v0:
```python
import math
import jax
import jax.numpy as jnp
from jax import lax
from jax.sharding import PartitionSpec as P

EPSILON = 1e-06
NEGATIVE = -1e30


def normed(tensor, gain_vector, rescale_factor):
    widened = tensor.astype(jnp.float32)
    inverse = lax.rsqrt(jnp.mean(widened * widened, axis=-1, keepdims=True) + EPSILON)
    return (widened * inverse * gain_vector * rescale_factor).astype(jnp.bfloat16)


def fragment_contributions(queries, key_rows, value_rows, valid):
    scores = jnp.einsum("qhd,khd->hqk", queries, key_rows, preferred_element_type=jnp.float32)
    if valid is not None:
        scores = jnp.where(valid[None, None, :], scores, NEGATIVE)
    maxima = jnp.max(scores, axis=-1)
    weights = jnp.exp(scores - maxima[..., None])
    if valid is not None:
        weights = jnp.where(valid[None, None, :], weights, 0.0)
    totals = jnp.sum(weights, axis=-1)
    accum = jnp.einsum(
        "hqk,khd->hqd", weights, value_rows.astype(jnp.float32), precision=lax.Precision.HIGHEST
    )
    return (maxima, totals, accum)


def combine(earlier, later):
    max_one, total_one, accum_one = earlier
    max_two, total_two, accum_two = later
    merged_max = jnp.maximum(max_one, max_two)
    factor_one = jnp.exp(max_one - merged_max)
    factor_two = jnp.exp(max_two - merged_max)
    merged_total = total_one * factor_one + total_two * factor_two
    merged_accum = accum_one * factor_one[..., None] + accum_two * factor_two[..., None]
    return (merged_max, merged_total, merged_accum)


def on_device(
    footage_probes,
    footage_lookup_keys,
    footage_payload,
    caption_probes,
    caption_lookup_keys,
    caption_payload,
    footage_probes_amplitude,
    footage_keys_amplitude,
    caption_probes_amplitude,
    caption_keys_amplitude,
    focus_sharpness,
    caption_validity,
):
    channel_width = footage_probes.shape[2]
    rescale_factor = focus_sharpness[None, :, None] / math.sqrt(channel_width)
    q_norm = normed(footage_probes, footage_probes_amplitude, rescale_factor)
    k_norm = normed(footage_lookup_keys, footage_keys_amplitude, 1.0)
    q_local = lax.all_to_all(q_norm, "blk", split_axis=1, concat_axis=0, tiled=True)
    k_local = lax.all_to_all(k_norm, "blk", split_axis=1, concat_axis=0, tiled=True)
    v_local = lax.all_to_all(footage_payload, "blk", split_axis=1, concat_axis=0, tiled=True)
    local_heads = q_local.shape[1]
    head_start = lax.axis_index("blk") * local_heads
    local_scale = lax.dynamic_slice_in_dim(rescale_factor, head_start, local_heads, 1)
    text_q = normed(
        lax.dynamic_slice_in_dim(caption_probes, head_start, local_heads, 1),
        caption_probes_amplitude,
        local_scale,
    )
    text_k = normed(
        lax.dynamic_slice_in_dim(caption_lookup_keys, head_start, local_heads, 1),
        caption_keys_amplitude,
        1.0,
    )
    text_v = lax.dynamic_slice_in_dim(caption_payload, head_start, local_heads, 1)
    text_valid = caption_validity == 1
    text_share = caption_probes.shape[0] // lax.axis_size("uly")
    row_start = lax.axis_index("uly") * text_share
    video_rows = q_local.shape[0]
    queries = jnp.concatenate(
        [q_local, lax.dynamic_slice_in_dim(text_q, row_start, text_share, 0)], 0
    )

    def fold_inward(running, gathered):
        key_block, value_block = gathered
        row_count = key_block.shape[0]
        block_rows = math.gcd(row_count, 512)

        def absorb_block(block_index, running_state):
            key_part = lax.dynamic_slice_in_dim(key_block, block_index * block_rows, block_rows, 0)
            value_part = lax.dynamic_slice_in_dim(
                value_block, block_index * block_rows, block_rows, 0
            )
            return combine(
                running_state, fragment_contributions(queries, key_part, value_part, None)
            )

        return lax.fori_loop(0, row_count // block_rows, absorb_block, running)

    first_state = fragment_contributions(queries, text_k, text_v, text_valid)
    maxima, totals, accum = fold_inward(
        first_state,
        (
            lax.all_gather(k_local, "uly", axis=0, tiled=True),
            lax.all_gather(v_local, "uly", axis=0, tiled=True),
        ),
    )
    attended = jnp.transpose(accum / totals[..., None], (1, 0, 2)).astype(jnp.bfloat16)
    vid_out = lax.all_to_all(attended[:video_rows], "blk", split_axis=0, concat_axis=1, tiled=True)
    txt_out = attended[video_rows:]
    return (vid_out, txt_out)


def solution(mesh):
    return jax.shard_map(
        on_device,
        mesh=mesh,
        in_specs=(
            P(("blk", "uly"), None, None),
            P(("blk", "uly"), None, None),
            P(("blk", "uly"), None, None),
            P(),
            P(),
            P(),
            P(),
            P(),
            P(),
            P(),
            P(),
            P(),
        ),
        out_specs=(P(("blk", "uly"), None, None), P("uly", "blk", None)),
        check_vma=False,
    )
```

profile of v0, /device:TPU:0, one launch (start us, length us, event | category | flops | bytes accessed | tf_op | source)
XLA Modules:
  0.0 76.9 jit_solution(12764766947317799488)
XLA Ops:
  0.7 0.8 broadcast_multiply_fusion
  1.4 1.2 %fusion.21 = f32[32,32]{0,1:T(8,128)S(1)} fusion(bf16[32,32,64]{2,1,0:T(8,128)(2,1)} %param.14), kind=kLoop, calls=%fused_computation.27 | loop fusion | flops 195584 | bytes 135168 | tf_op jit(solution)/shard_map/reduce_sum | solution.py:13
  2.6 1.2 %fusion.44 = bf16[32,32,64]{2,1,0:T(8,128)(2,1)S(1)} fusion(f32[32]{0:T(128)S(1)} %broadcast_multiply_fusion, f32[64]{0:T(128)} %param.20, f32[32,32]{0,1:T(8,128)S(1)} %add_rsqrt_fusion.1, bf16[32,32,64]{2,1,0:T(8,128)(2,1)} %param.14), kind=kLoop, calls=%fused_computation.64 | loop fusion | flops 327680 | bytes 266624
  3.8 0.9 %reshape.50 = bf16[16,2,2048]{2,1,0:T(2,128)(2,1)} reshape(bf16[32,32,64]{2,1,0:T(8,128)(2,1)S(1)} %fusion.44) | data formatting | bytes 262144
  4.7 7.4 %all-to-all-start = ((bf16[16,2,2048]{2,1,0:T(2,128)(2,1)}), bf16[16,2,2048]{2,1,0:T(2,128)(2,1)S(1)}, u32[]{:S(2)}, u32[]{:S(2)}) async-start(bf16[16,2,2048]{2,1,0:T(2,128)(2,1)} %reshape.50), calls=%async_computation | async-start | bytes 262144 | tf_op jit(solution)/shard_map/all_to_all | solution.py:61
  12.2 0.9 %fusion.28 = (f32[256,2]{0,1:T(2,128)S(1)}, f32[256,2]{0,1:T(2,128)S(1)}) fusion(bf16[256,32,64]{0,2,1:T(8,128)(2,1)} %param.18, s32[]{:T(128)S(6)} %select_n.24, bf16[256,32,64]{0,2,1:T(8,128)(2,1)} %param.17), kind=kLoop, calls=%fused_computation.38 | loop fusion | flops 195584 | bytes 135172 | tf_op jit(solution)/shard_map/reduce_sum | solution.py:13
  13.1 0.2 fusion.25
  13.6 0.9 %dynamic-slice_convert_fusion = f32[256,2,64]{0,2,1:T(8,128)S(1)} fusion(bf16[256,32,64]{0,2,1:T(8,128)(2,1)} %param.17, s32[]{:T(128)S(6)} %select_n.24), kind=kLoop, calls=%fused_computation.49 | loop fusion | flops 32768 | bytes 196612 | tf_op jit(solution)/shard_map/convert_element_type | solution.py:12
  14.5 0.9 %reshape.52 = bf16[16,2,2048]{2,1,0:T(2,128)(2,1)} reshape(bf16[32,32,64]{2,1,0:T(8,128)(2,1)S(1)} %fusion.43) | data formatting | bytes 262144
  15.3 4.7 %all-to-all-done = bf16[16,2,2048]{2,1,0:T(2,128)(2,1)S(1)} async-done(((bf16[16,2,2048]{2,1,0:T(2,128)(2,1)}), bf16[16,2,2048]{2,1,0:T(2,128)(2,1)S(1)}, u32[]{:S(2)}, u32[]{:S(2)}) %all-to-all-start) | async-done | bytes 131104 | tf_op jit(solution)/shard_map/all_to_all | solution.py:61
  20.1 3.5 %all-to-all-start.1 = ((bf16[16,2,2048]{2,1,0:T(2,128)(2,1)}), bf16[16,2,2048]{2,1,0:T(2,128)(2,1)S(1)}, u32[]{:S(2)}, u32[]{:S(2)}) async-start(bf16[16,2,2048]{2,1,0:T(2,128)(2,1)} %reshape.52), calls=%async_computation.1 | async-start | bytes 262144 | tf_op jit(solution)/shard_map/all_to_all | solution.py:62
  23.8 0.9 %reshape.54 = bf16[16,2,2048]{2,1,0:T(2,128)(2,1)} reshape(bf16[32,32,64]{2,1,0:T(8,128)(2,1)S(1)} %bitcast.58) | data formatting | bytes 262144
  24.8 6.7 %all-to-all-done.1 = bf16[16,2,2048]{2,1,0:T(2,128)(2,1)S(1)} async-done(((bf16[16,2,2048]{2,1,0:T(2,128)(2,1)}), bf16[16,2,2048]{2,1,0:T(2,128)(2,1)S(1)}, u32[]{:S(2)}, u32[]{:S(2)}) %all-to-all-start.1) | async-done | bytes 131104 | tf_op jit(solution)/shard_map/all_to_all | solution.py:62
  31.4 3.5 %all-to-all-start.2 = ((bf16[16,2,2048]{2,1,0:T(2,128)(2,1)}), bf16[16,2,2048]{2,1,0:T(2,128)(2,1)S(1)}, u32[]{:S(2)}, u32[]{:S(2)}) async-start(bf16[16,2,2048]{2,1,0:T(2,128)(2,1)} %reshape.54), calls=%async_computation.2 | async-start | bytes 262144 | tf_op jit(solution)/shard_map/all_to_all | solution.py:63
  35.6 9.2 %all_gather.6 = bf16[1024,2,64]{2,0,1:T(8,128)(2,1)S(1)} all-gather(bf16[512,2,64]{2,0,1:T(8,128)(2,1)S(1)} %bitcast.50), channel_id=1, replica_groups=mesh['blk'=16,'uly'=2] {'uly'}, dimensions={0}, use_global_device_ids=true | all-gather | bytes 393216 | tf_op jit(solution)/shard_map/all_gather | solution.py:106
  45.2 8.3 %all_gather.7 = bf16[1024,2,64]{2,0,1:T(8,128)(2,1)S(1)} all-gather(bf16[512,2,64]{2,0,1:T(8,128)(2,1)S(1)} %bitcast.51), channel_id=1, replica_groups=mesh['blk'=16,'uly'=2] {'uly'}, dimensions={0}, use_global_device_ids=true | all-gather | bytes 393216 | tf_op jit(solution)/shard_map/all_gather | solution.py:107
  53.8 1.3 %fusion.42 = (f32[2,640]{1,0:T(2,128)S(1)}, f32[2,640,256]{1,2,0:T(8,128)S(1)}) fusion(f32[64]{0:T(128)S(1)} %copy-done.5, f32[256,2]{0,1:T(2,128)S(1)} %add_rsqrt_fusion.2, bf16[256,32,64]{0,2,1:T(8,128)(2,1)} %param.18, s32[]{:T(128)S(6)} %select_n.24, bf16[128,2,64]{0,2,1:T(8,128)(2,1)S(1)} %fusion.34, bf16[512,2,64]{0,2,1:T(8,128)(2,1)S(1)} %copy.45, ...), kind=kOutput, calls=%fused_computation.61 | convolution fusion | flops 43055872 | bytes 1547780 | tf_op jit(solution)/shard_map/qhd,khd->hqk/dot_general | solution.py:18
  55.1 0.3 fusion.17
  55.4 0.8 %fusion.16 = f32[2,640,64]{1,2,0:T(8,128)S(1)} fusion(f32[2,640,256]{1,2,0:T(8,128)S(1)} %get-tuple-element.177, f32[2,640]{1,0:T(2,128)S(1)} %get-tuple-element.236, pred[256]{0:T(512)(128)(4,1)S(1)} %broadcast_compare_fusion, bf16[256,32,64]{0,2,1:T(8,128)(2,1)S(1)} %copy-done, s32[]{:T(128)S(6)} %select_n.24), kind=kOutput, calls=%fused_computation.18 | convolution fusion | flops 252313600 | bytes 1709572 | tf_op jit(solution)/shard_map/hqk,khd->hqd/dot_general | solution.py:26
  56.2 4.7 %while.17 = (s32[]{:T(128)}, f32[2,640]{1,0:T(2,128)S(1)}, f32[2,640]{1,0:T(2,128)S(1)}, f32[2,640,64]{1,2,0:T(8,128)S(1)}, bf16[1024,2,64]{0,2,1:T(8,128)(2,1)S...) while((s32[]{:T(128)}, f32[2,640]{1,0:T(2,128)S(1)}, ...), condition=%wide.region_9.10_spmd, body=%wide.region_6.9_spmd.sunk | while | flops 590074880 | bytes 9017507 | solution.py:100
  56.2 0.6 bitcast_reduce_fusion.2
  56.8 0.4 fusion.54
  57.2 1.4 %fusion.55 = f32[2,640,64]{1,2,0:T(8,128)S(1)} fusion(f32[2,512,640]{2,1,0:T(8,128)S(1)} %get-tuple-element.229, f32[2,640]{1,0:T(2,128)S(1)} %get-tuple-element.230, f32[2,640,64]{1,2,0:T(8,128)S(1)} %get-tuple-element.249, f32[2,640]{1,0:T(2,128)S(1)} %get-tuple-element.233, f32[2,640]{1,0:T(2,128)S(1)} %get-tuple-element.234, ...), kind=kOutput, calls=%fused_computation.7.clone.1 | convolution fusion | flops 504217600 | bytes 3423236 | tf_op jit(solution)/shard_map/while/body/eval_jaxpr/hqk,khd->hqd/dot_general | solution.py:26
  58.5 0.6 bitcast_reduce_fusion.2
  59.1 0.4 fusion.54
  59.5 1.3 %fusion.55 = f32[2,640,64]{1,2,0:T(8,128)S(1)} fusion(f32[2,512,640]{2,1,0:T(8,128)S(1)} %get-tuple-element.229, f32[2,640]{1,0:T(2,128)S(1)} %get-tuple-element.230, f32[2,640,64]{1,2,0:T(8,128)S(1)} %get-tuple-element.249, f32[2,640]{1,0:T(2,128)S(1)} %get-tuple-element.233, f32[2,640]{1,0:T(2,128)S(1)} %get-tuple-element.234, ...), kind=kOutput, calls=%fused_computation.7.clone.1 | convolution fusion | flops 504217600 | bytes 3423236 | tf_op jit(solution)/shard_map/while/body/eval_jaxpr/hqk,khd->hqd/dot_general | solution.py:26
  60.9 0.2 copy.55
  61.3 0.9 %reshape.56 = bf16[16,2,2048]{2,1,0:T(2,128)(2,1)} reshape(bf16[512,2,64]{2,1,0:T(2,128)(2,1)S(1)} %slice.8) | data formatting | bytes 262144
  62.2 5.6 %all-to-all-start.3 = ((bf16[16,2,2048]{2,1,0:T(2,128)(2,1)}), bf16[16,2,2048]{2,1,0:T(2,128)(2,1)S(1)}, u32[]{:S(2)}, u32[]{:S(2)}) async-start(bf16[16,2,2048]{2,1,0:T(2,128)(2,1)} %reshape.56), calls=%async_computation.3 | async-start | bytes 262144 | tf_op jit(solution)/shard_map/all_to_all | solution.py:111
  67.9 0.7 copy.59
  68.6 7.1 %all-to-all-done.3 = bf16[16,2,2048]{2,1,0:T(2,128)(2,1)S(1)} async-done(((bf16[16,2,2048]{2,1,0:T(2,128)(2,1)}), bf16[16,2,2048]{2,1,0:T(2,128)(2,1)S(1)}, u32[]{:S(2)}, u32[]{:S(2)}) %all-to-all-start.3) | async-done | bytes 131104 | tf_op jit(solution)/shard_map/all_to_all | solution.py:111
  76.1 0.8 %copy.58 = bf16[32,32,64]{2,1,0:T(8,128)(2,1)} copy(bf16[32,32,64]{2,0,1:T(8,128)(2,1)S(1)} %bitcast.57) | data formatting | bytes 262144
  (43 shorter events, 2.4 us)
Async XLA Ops:
  0.6 54.7 %copy-start = (bf16[256,32,64]{0,2,1:T(8,128)(2,1)S(1)}, bf16[256,32,64]{0,2,1:T(8,128)(2,1)}, u32[]{:S(2)}) copy-start(bf16[256,32,64]{0,2,1:T(8,128)(2,1)} %param.19) | copy-start | bytes 3145732
  0.6 12.4 %copy-start.1 = (bf16[32,32,64]{2,1,0:T(8,128)(2,1)S(1)}, bf16[32,32,64]{2,1,0:T(8,128)(2,1)}, u32[]{:S(2)}) copy-start(bf16[32,32,64]{2,1,0:T(8,128)(2,1)} %param.15) | copy-start | bytes 393220
  0.7 12.7 %copy-start.3 = (f32[64]{0:T(128)S(1)}, f32[64]{0:T(128)}, u32[]{:S(2)}) copy-start(f32[64]{0:T(128)} %param.21) | copy-start | bytes 772
  3.8 19.9 %copy-start.2 = (bf16[32,32,64]{2,1,0:T(8,128)(2,1)S(1)}, bf16[32,32,64]{2,1,0:T(8,128)(2,1)}, u32[]{:S(2)}) copy-start(bf16[32,32,64]{2,1,0:T(8,128)(2,1)} %param.16) | copy-start | bytes 393220
  4.7 15.3 %all-to-all-start = ((bf16[16,2,2048]{2,1,0:T(2,128)(2,1)}), bf16[16,2,2048]{2,1,0:T(2,128)(2,1)S(1)}, u32[]{:S(2)}, u32[]{:S(2)}) async-start(bf16[16,2,2048]{2,1,0:T(2,128)(2,1)} %reshape.50), calls=%async_computation | async-start | bytes 262144 | tf_op jit(solution)/shard_map/all_to_all | solution.py:61
  13.1 11.6 %copy-start.4 = (f32[64]{0:T(128)S(1)}, f32[64]{0:T(128)}, u32[]{:S(2)}) copy-start(f32[64]{0:T(128)} %param.22) | copy-start | bytes 772
  13.4 21.6 %copy-start.6 = (s32[256]{0:T(256)S(1)}, s32[256]{0:T(256)}, u32[]{:S(2)}) copy-start(s32[256]{0:T(256)} %param.25) | copy-start | bytes 3076
  20.1 11.4 %all-to-all-start.1 = ((bf16[16,2,2048]{2,1,0:T(2,128)(2,1)}), bf16[16,2,2048]{2,1,0:T(2,128)(2,1)S(1)}, u32[]{:S(2)}, u32[]{:S(2)}) async-start(bf16[16,2,2048]{2,1,0:T(2,128)(2,1)} %reshape.52), calls=%async_computation.1 | async-start | bytes 262144 | tf_op jit(solution)/shard_map/all_to_all | solution.py:62
  31.4 13.5 %all-to-all-start.2 = ((bf16[16,2,2048]{2,1,0:T(2,128)(2,1)}), bf16[16,2,2048]{2,1,0:T(2,128)(2,1)S(1)}, u32[]{:S(2)}, u32[]{:S(2)}) async-start(bf16[16,2,2048]{2,1,0:T(2,128)(2,1)} %reshape.54), calls=%async_computation.2 | async-start | bytes 262144 | tf_op jit(solution)/shard_map/all_to_all | solution.py:63
  45.2 8.6 %copy-start.5 = (f32[64]{0:T(128)S(1)}, f32[64]{0:T(128)}, u32[]{:S(2)}) copy-start(f32[64]{0:T(128)} %param.23) | copy-start | bytes 772
  62.2 13.6 %all-to-all-start.3 = ((bf16[16,2,2048]{2,1,0:T(2,128)(2,1)}), bf16[16,2,2048]{2,1,0:T(2,128)(2,1)S(1)}, u32[]{:S(2)}, u32[]{:S(2)}) async-start(bf16[16,2,2048]{2,1,0:T(2,128)(2,1)} %reshape.56), calls=%async_computation.3 | async-start | bytes 262144 | tf_op jit(solution)/shard_map/all_to_all | solution.py:111
where the time goes:
time: 77.5 us; the launch traced here: 76.9 us
  starting transfers between devices  20.1 us (26%)
  waiting for transfers between devices  18.5 us (24%)
  blocking collectives  17.5 us (23%)
  local copies, waits for them, and re-layouts  7.24 us (9%)
  other arithmetic  6.54 us (8%)
  matrix products  5.96 us (8%)
  between operations  1 us (1%)
    all_gather x1, blocking collectives, on_device(): lax.all_gather(k_local, 'uly', axis=0, tiled=True)  9.16 us
    all_gather x1, blocking collectives, on_device(): lax.all_gather(v_local, 'uly', axis=0, tiled=True)  8.3 us
    all_to_all x1, starting transfers between devices, on_device(): lax.all_to_all(q_norm, 'blk', split_axis=1, concat_axis=0, tiled=True)  7.41 us
    all_to_all x1, waiting for transfers between devices, on_device(): lax.all_to_all(attended[:video_rows], 'blk', split_axis=0, concat_axis=1,...  7.13 us
    all_to_all x1, waiting for transfers between devices, on_device(): lax.all_to_all(k_norm, 'blk', split_axis=1, concat_axis=0, tiled=True)  6.68 us
    unnamed x25, local copies, waits for them, and re-layouts  6.08 us
    all_to_all x1, starting transfers between devices, on_device(): lax.all_to_all(attended[:video_rows], 'blk', split_axis=0, concat_axis=1,...  5.64 us
    all_to_all x1, waiting for transfers between devices, on_device(): lax.all_to_all(q_norm, 'blk', split_axis=1, concat_axis=0, tiled=True)  4.72 us
  transfers between devices with their start and end apart: 4, of which 3 were waited for; matrix products, arithmetic and copies ran while one was open for 8% of the time, Pallas kernels for 0%

commit v1 on v0

--- a/solution.py
+++ b/solution.py
@@ -58,7 +58,10 @@
     rescale_factor = focus_sharpness[None, :, None] / math.sqrt(channel_width)
     q_norm = normed(footage_probes, footage_probes_amplitude, rescale_factor)
     k_norm = normed(footage_lookup_keys, footage_keys_amplitude, 1.0)
-    q_local = lax.all_to_all(q_norm, "blk", split_axis=1, concat_axis=0, tiled=True)
+    q_local = jnp.concatenate(
+        lax.all_to_all(jnp.stack(jnp.split(q_norm, lax.axis_size("blk"), axis=1)), "blk", 0, 0),
+        axis=0,
+    )
     k_local = lax.all_to_all(k_norm, "blk", split_axis=1, concat_axis=0, tiled=True)
     v_local = lax.all_to_all(footage_payload, "blk", split_axis=1, concat_axis=0, tiled=True)
     local_heads = q_local.shape[1]

time: 77.5 us -> 77.1 us (level)
  waiting for transfers between devices: 18.5 us -> 17.2 us
    all_to_all x1, starting transfers between devices: 3.51 us -> 7.55 us  [on_device(): lax.all_to_all(k_norm, 'blk', split_axis=1, concat_axis=0, tiled=True)]
    all_to_all x1, starting transfers between devices: 7.41 us -> 3.51 us  [on_device(): lax.all_to_all(jnp.stack(jnp.split(q_norm, lax.axis_size('blk'), axis=1))...]
    all_to_all x1, waiting for transfers between devices: 6.68 us -> 3.37 us  [on_device(): lax.all_to_all(k_norm, 'blk', split_axis=1, concat_axis=0, tiled=True)]
    all_to_all x1, waiting for transfers between devices: 4.72 us -> 6.7 us  [on_device(): lax.all_to_all(jnp.stack(jnp.split(q_norm, lax.axis_size('blk'), axis=1))...]
    reduce_sum x3 -> x4, other arithmetic: 2.3 us -> 3.22 us  [normed(): jnp.mean(widened * widened, axis=-1, keepdims=True) + EPSILON]
    unnamed x25 -> x42, local copies, waits for them, and re-layouts: 6.08 us -> 6.48 us
  transfers between devices with their start and end apart: 4 -> 4, of which waited for: 3 -> 3; matrix products, arithmetic and copies ran while one was open for 8% -> 9% of each run, Pallas kernels for 0% -> 0%
where the time goes in v1:
time: 77.1 us; the launch traced here: 76.4 us
  starting transfers between devices  20.2 us (26%)
  blocking collectives  17.5 us (23%)
  waiting for transfers between devices  17.2 us (22%)
  local copies, waits for them, and re-layouts  7.82 us (10%)
  other arithmetic  6.69 us (9%)
  matrix products  5.96 us (8%)
  between operations  1.03 us (1%)
    all_gather x1, blocking collectives, on_device(): lax.all_gather(k_local, 'uly', axis=0, tiled=True)  9.16 us
    all_gather x1, blocking collectives, on_device(): lax.all_gather(v_local, 'uly', axis=0, tiled=True)  8.3 us
    all_to_all x1, starting transfers between devices, on_device(): lax.all_to_all(k_norm, 'blk', split_axis=1, concat_axis=0, tiled=True)  7.55 us
    all_to_all x1, waiting for transfers between devices, on_device(): lax.all_to_all(attended[:video_rows], 'blk', split_axis=0, concat_axis=1,...  7.13 us
    all_to_all x1, waiting for transfers between devices, on_device(): lax.all_to_all(jnp.stack(jnp.split(q_norm, lax.axis_size('blk'), axis=1))...  6.7 us
    unnamed x42, local copies, waits for them, and re-layouts  6.48 us
    all_to_all x1, starting transfers between devices, on_device(): lax.all_to_all(attended[:video_rows], 'blk', split_axis=0, concat_axis=1,...  5.64 us
    all_to_all x1, starting transfers between devices, on_device(): lax.all_to_all(jnp.stack(jnp.split(q_norm, lax.axis_size('blk'), axis=1))...  3.51 us
  transfers between devices with their start and end apart: 4, of which 3 were waited for; matrix products, arithmetic and copies ran while one was open for 9% of the time, Pallas kernels for 0%

profile of v1, /device:TPU:0, one launch (start us, length us, event | category | flops | bytes accessed | tf_op | source)
XLA Modules:
  0.0 76.4 jit_solution(10184962702147283171)
XLA Ops:
  0.7 1.3 %fusion.25 = f32[32,32]{0,1:T(8,128)S(1)} fusion(bf16[32,32,64]{2,1,0:T(8,128)(2,1)} %param.15), kind=kLoop, calls=%fused_computation.31 | loop fusion | flops 195584 | bytes 135168 | tf_op jit(solution)/shard_map/reduce_sum | solution.py:13
  2.1 1.2 %fusion.43 = bf16[32,32,64]{2,1,0:T(8,128)(2,1)S(1)} fusion(f32[64]{0:T(128)} %param.21, f32[32,32]{0,1:T(8,128)S(1)} %copy.84, bf16[32,32,64]{2,1,0:T(8,128)(2,1)} %param.15), kind=kLoop, calls=%fused_computation.94 | loop fusion | flops 262144 | bytes 266496
  3.3 0.9 %reshape.56 = bf16[16,2,2048]{2,1,0:T(2,128)(2,1)} reshape(bf16[32,32,64]{2,1,0:T(8,128)(2,1)S(1)} %fusion.43) | data formatting | bytes 262144
  4.2 7.5 %all-to-all-start.1 = ((bf16[16,2,2048]{2,1,0:T(2,128)(2,1)}), bf16[16,2,2048]{2,1,0:T(2,128)(2,1)S(1)}, u32[]{:S(2)}, u32[]{:S(2)}) async-start(bf16[16,2,2048]{2,1,0:T(2,128)(2,1)} %reshape.56), calls=%async_computation.1 | async-start | bytes 262144 | tf_op jit(solution)/shard_map/all_to_all | solution.py:65
  11.8 0.9 %multiply_reduce_fusion = f32[256,2]{0,1:T(2,128)S(1)} fusion(bf16[256,32,64]{0,2,1:T(8,128)(2,1)} %param.17, s32[]{:T(128)S(6)} %select_n.24), kind=kLoop, calls=%fused_computation.41 | loop fusion | flops 97792 | bytes 67588 | tf_op jit(solution)/shard_map/reduce_sum | solution.py:13
  12.9 0.2 fusion.24
  13.6 0.9 %dynamic-slice_convert_fusion = f32[256,2,64]{0,2,1:T(8,128)S(1)} fusion(bf16[256,32,64]{0,2,1:T(8,128)(2,1)} %param.17, s32[]{:T(128)S(6)} %select_n.24), kind=kLoop, calls=%fused_computation.49 | loop fusion | flops 32768 | bytes 196612 | tf_op jit(solution)/shard_map/convert_element_type | solution.py:12
  14.5 0.9 %reshape.54 = bf16[16,2,2048]{2,1,0:T(2,128)(2,1)} reshape(bf16[16,32,2,64]{3,2,1,0:T(2,128)(2,1)S(1)} %constant_dynamic-update-slice_fusion) | data formatting | bytes 262144
  15.4 0.9 %fusion.28 = f32[256,2]{0,1:T(2,128)S(1)} fusion(bf16[256,32,64]{0,2,1:T(8,128)(2,1)} %param.18, s32[]{:T(128)S(6)} %select_n.24), kind=kLoop, calls=%fused_computation.38 | loop fusion | flops 97792 | bytes 67588 | tf_op jit(solution)/shard_map/reduce_sum | solution.py:13
  16.3 3.4 %all-to-all-done.1 = bf16[16,2,2048]{2,1,0:T(2,128)(2,1)S(1)} async-done(((bf16[16,2,2048]{2,1,0:T(2,128)(2,1)}), bf16[16,2,2048]{2,1,0:T(2,128)(2,1)S(1)}, u32[]{:S(2)}, u32[]{:S(2)}) %all-to-all-start.1) | async-done | bytes 131104 | tf_op jit(solution)/shard_map/all_to_all | solution.py:65
  19.6 3.5 %all-to-all-start = ((bf16[16,2,2048]{2,1,0:T(2,128)(2,1)}), bf16[16,2,2048]{2,1,0:T(2,128)(2,1)S(1)}, u32[]{:S(2)}, u32[]{:S(2)}) async-start(bf16[16,2,2048]{2,1,0:T(2,128)(2,1)} %reshape.54), calls=%async_computation | async-start | bytes 262144 | tf_op jit(solution)/shard_map/all_to_all | solution.py:62
  23.4 0.9 %reshape.58 = bf16[16,2,2048]{2,1,0:T(2,128)(2,1)} reshape(bf16[32,32,64]{2,1,0:T(8,128)(2,1)S(1)} %bitcast.115) | data formatting | bytes 262144
  24.3 6.7 %all-to-all-done = bf16[16,2,2048]{2,1,0:T(2,128)(2,1)S(1)} async-done(((bf16[16,2,2048]{2,1,0:T(2,128)(2,1)}), bf16[16,2,2048]{2,1,0:T(2,128)(2,1)S(1)}, u32[]{:S(2)}, u32[]{:S(2)}) %all-to-all-start) | async-done | bytes 131104 | tf_op jit(solution)/shard_map/all_to_all | solution.py:62
  31.0 3.5 %all-to-all-start.2 = ((bf16[16,2,2048]{2,1,0:T(2,128)(2,1)}), bf16[16,2,2048]{2,1,0:T(2,128)(2,1)S(1)}, u32[]{:S(2)}, u32[]{:S(2)}) async-start(bf16[16,2,2048]{2,1,0:T(2,128)(2,1)} %reshape.58), calls=%async_computation.2 | async-start | bytes 262144 | tf_op jit(solution)/shard_map/all_to_all | solution.py:66
  34.8 9.2 %all_gather.6 = bf16[1024,2,64]{2,0,1:T(8,128)(2,1)S(1)} all-gather(bf16[512,2,64]{2,0,1:T(8,128)(2,1)S(1)} %bitcast.108), channel_id=1, replica_groups=mesh['blk'=16,'uly'=2] {'uly'}, dimensions={0}, use_global_device_ids=true | all-gather | bytes 393216 | tf_op jit(solution)/shard_map/all_gather | solution.py:109
  44.8 8.3 %all_gather.7 = bf16[1024,2,64]{2,0,1:T(8,128)(2,1)S(1)} all-gather(bf16[512,2,64]{2,0,1:T(8,128)(2,1)S(1)} %bitcast.109), channel_id=1, replica_groups=mesh['blk'=16,'uly'=2] {'uly'}, dimensions={0}, use_global_device_ids=true | all-gather | bytes 393216 | tf_op jit(solution)/shard_map/all_gather | solution.py:110
  53.3 1.3 %fusion.42 = (f32[2,640]{1,0:T(2,128)S(1)}, f32[2,640,256]{1,2,0:T(8,128)S(1)}) fusion(f32[64]{0:T(128)S(1)} %copy-done.4, f32[256,2]{0,1:T(2,128)S(1)} %add_rsqrt_fusion.2, bf16[256,32,64]{0,2,1:T(8,128)(2,1)} %param.18, s32[]{:T(128)S(6)} %select_n.24, bf16[128,2,64]{0,2,1:T(8,128)(2,1)S(1)} %fusion.34, bf16[512,2,64]{0,2,1:T(8,128)(2,1)S(1)} %copy.80, ...), kind=kOutput, calls=%fused_computation.93 | convolution fusion | flops 43055872 | bytes 1547780 | tf_op jit(solution)/shard_map/qhd,khd->hqk/dot_general | solution.py:18
  54.6 0.3 fusion.17
  54.9 0.8 %fusion.16 = f32[2,640,64]{1,2,0:T(8,128)S(1)} fusion(f32[2,640,256]{1,2,0:T(8,128)S(1)} %get-tuple-element.195, f32[2,640]{1,0:T(2,128)S(1)} %get-tuple-element.252, pred[256]{0:T(512)(128)(4,1)S(1)} %broadcast_compare_fusion, bf16[256,32,64]{0,2,1:T(8,128)(2,1)S(1)} %copy-done, s32[]{:T(128)S(6)} %select_n.24), kind=kOutput, calls=%fused_computation.18 | convolution fusion | flops 252313600 | bytes 1709572 | tf_op jit(solution)/shard_map/hqk,khd->hqd/dot_general | solution.py:26
  55.7 4.7 %while.17 = (s32[]{:T(128)}, f32[2,640]{1,0:T(2,128)S(1)}, f32[2,640]{1,0:T(2,128)S(1)}, f32[2,640,64]{1,2,0:T(8,128)S(1)}, bf16[1024,2,64]{0,2,1:T(8,128)(2,1)S...) while((s32[]{:T(128)}, f32[2,640]{1,0:T(2,128)S(1)}, ...), condition=%wide.region_9.10_spmd, body=%wide.region_6.9_spmd.sunk | while | flops 590074880 | bytes 9017507 | solution.py:103
  55.8 0.6 bitcast_reduce_fusion.2
  56.3 0.4 fusion.53
  56.7 1.3 %fusion.54 = f32[2,640,64]{1,2,0:T(8,128)S(1)} fusion(f32[2,512,640]{2,1,0:T(8,128)S(1)} %get-tuple-element.245, f32[2,640]{1,0:T(2,128)S(1)} %get-tuple-element.246, f32[2,640,64]{1,2,0:T(8,128)S(1)} %get-tuple-element.265, f32[2,640]{1,0:T(2,128)S(1)} %get-tuple-element.249, f32[2,640]{1,0:T(2,128)S(1)} %get-tuple-element.250, ...), kind=kOutput, calls=%fused_computation.7.clone.1 | convolution fusion | flops 504217600 | bytes 3423236 | tf_op jit(solution)/shard_map/while/body/eval_jaxpr/hqk,khd->hqd/dot_general | solution.py:26
  58.1 0.6 bitcast_reduce_fusion.2
  58.7 0.4 fusion.53
  59.1 1.3 %fusion.54 = f32[2,640,64]{1,2,0:T(8,128)S(1)} fusion(f32[2,512,640]{2,1,0:T(8,128)S(1)} %get-tuple-element.245, f32[2,640]{1,0:T(2,128)S(1)} %get-tuple-element.246, f32[2,640,64]{1,2,0:T(8,128)S(1)} %get-tuple-element.265, f32[2,640]{1,0:T(2,128)S(1)} %get-tuple-element.249, f32[2,640]{1,0:T(2,128)S(1)} %get-tuple-element.250, ...), kind=kOutput, calls=%fused_computation.7.clone.1 | convolution fusion | flops 504217600 | bytes 3423236 | tf_op jit(solution)/shard_map/while/body/eval_jaxpr/hqk,khd->hqd/dot_general | solution.py:26
  60.5 0.2 copy.92
  60.9 0.9 %reshape.60 = bf16[16,2,2048]{2,1,0:T(2,128)(2,1)} reshape(bf16[512,2,64]{2,1,0:T(2,128)(2,1)S(1)} %slice.8) | data formatting | bytes 262144
  61.8 5.6 %all-to-all-start.3 = ((bf16[16,2,2048]{2,1,0:T(2,128)(2,1)}), bf16[16,2,2048]{2,1,0:T(2,128)(2,1)S(1)}, u32[]{:S(2)}, u32[]{:S(2)}) async-start(bf16[16,2,2048]{2,1,0:T(2,128)(2,1)} %reshape.60), calls=%async_computation.3 | async-start | bytes 262144 | tf_op jit(solution)/shard_map/all_to_all | solution.py:114
  67.5 0.7 copy.96
  68.2 7.1 %all-to-all-done.3 = bf16[16,2,2048]{2,1,0:T(2,128)(2,1)S(1)} async-done(((bf16[16,2,2048]{2,1,0:T(2,128)(2,1)}), bf16[16,2,2048]{2,1,0:T(2,128)(2,1)S(1)}, u32[]{:S(2)}, u32[]{:S(2)}) %all-to-all-start.3) | async-done | bytes 131104 | tf_op jit(solution)/shard_map/all_to_all | solution.py:114
  75.6 0.8 %copy.95 = bf16[32,32,64]{2,1,0:T(8,128)(2,1)} copy(bf16[32,32,64]{2,0,1:T(8,128)(2,1)S(1)} %bitcast.114) | data formatting | bytes 262144
  (63 shorter events, 3.0 us)
Async XLA Ops:
  0.6 54.3 %copy-start = (bf16[256,32,64]{0,2,1:T(8,128)(2,1)S(1)}, bf16[256,32,64]{0,2,1:T(8,128)(2,1)}, u32[]{:S(2)}) copy-start(bf16[256,32,64]{0,2,1:T(8,128)(2,1)} %param.19) | copy-start | bytes 3145732
  0.6 11.1 %copy-start.7 = (f32[32]{0:T(128)S(1)}, f32[32]{0:T(128)}, u32[]{:S(2)}) copy-start(f32[32]{0:T(128)} %param.24) | copy-start | bytes 388
  0.7 12.0 %copy-start.1 = (bf16[32,32,64]{2,1,0:T(8,128)(2,1)S(1)}, bf16[32,32,64]{2,1,0:T(8,128)(2,1)}, u32[]{:S(2)}) copy-start(bf16[32,32,64]{2,1,0:T(8,128)(2,1)} %param.14) | copy-start | bytes 393220
  0.7 12.2 %copy-start.5 = (f32[64]{0:T(128)S(1)}, f32[64]{0:T(128)}, u32[]{:S(2)}) copy-start(f32[64]{0:T(128)} %param.20) | copy-start | bytes 772
  4.2 19.1 %copy-start.2 = (bf16[32,32,64]{2,1,0:T(8,128)(2,1)S(1)}, bf16[32,32,64]{2,1,0:T(8,128)(2,1)}, u32[]{:S(2)}) copy-start(bf16[32,32,64]{2,1,0:T(8,128)(2,1)} %param.16) | copy-start | bytes 393220
  4.2 15.5 %all-to-all-start.1 = ((bf16[16,2,2048]{2,1,0:T(2,128)(2,1)}), bf16[16,2,2048]{2,1,0:T(2,128)(2,1)S(1)}, u32[]{:S(2)}, u32[]{:S(2)}) async-start(bf16[16,2,2048]{2,1,0:T(2,128)(2,1)} %reshape.56), calls=%async_computation.1 | async-start | bytes 262144 | tf_op jit(solution)/shard_map/all_to_all | solution.py:65
  13.1 11.1 %copy-start.3 = (f32[64]{0:T(128)S(1)}, f32[64]{0:T(128)}, u32[]{:S(2)}) copy-start(f32[64]{0:T(128)} %param.22) | copy-start | bytes 772
  13.2 21.3 %copy-start.6 = (s32[256]{0:T(256)S(1)}, s32[256]{0:T(256)}, u32[]{:S(2)}) copy-start(s32[256]{0:T(256)} %param.25) | copy-start | bytes 3076
  19.6 11.4 %all-to-all-start = ((bf16[16,2,2048]{2,1,0:T(2,128)(2,1)}), bf16[16,2,2048]{2,1,0:T(2,128)(2,1)S(1)}, u32[]{:S(2)}, u32[]{:S(2)}) async-start(bf16[16,2,2048]{2,1,0:T(2,128)(2,1)} %reshape.54), calls=%async_computation | async-start | bytes 262144 | tf_op jit(solution)/shard_map/all_to_all | solution.py:62
  31.0 13.5 %all-to-all-start.2 = ((bf16[16,2,2048]{2,1,0:T(2,128)(2,1)}), bf16[16,2,2048]{2,1,0:T(2,128)(2,1)S(1)}, u32[]{:S(2)}, u32[]{:S(2)}) async-start(bf16[16,2,2048]{2,1,0:T(2,128)(2,1)} %reshape.58), calls=%async_computation.2 | async-start | bytes 262144 | tf_op jit(solution)/shard_map/all_to_all | solution.py:66
  44.8 8.6 %copy-start.4 = (f32[64]{0:T(128)S(1)}, f32[64]{0:T(128)}, u32[]{:S(2)}) copy-start(f32[64]{0:T(128)} %param.23) | copy-start | bytes 772
  61.8 13.6 %all-to-all-start.3 = ((bf16[16,2,2048]{2,1,0:T(2,128)(2,1)}), bf16[16,2,2048]{2,1,0:T(2,128)(2,1)S(1)}, u32[]{:S(2)}, u32[]{:S(2)}) async-start(bf16[16,2,2048]{2,1,0:T(2,128)(2,1)} %reshape.60), calls=%async_computation.3 | async-start | bytes 262144 | tf_op jit(solution)/shard_map/all_to_all | solution.py:114
